TPU v7x, 256 devices: a whole 4x4x8 slice. The times are simulated.
256 devices in a mesh: dp: 8 (over y, core), vocab: 32 (over x, z).
Axes of the slice: x: 4, y: 4, z: 8, core: 2. Of those that a mesh axis runs over, the one named last changes fastest.
Arguments:
- student_hidden: bfloat16 [4096, 2048], P('dp', 'vocab'), may hold values from -150 to 150
- teacher_hidden: bfloat16 [4096, 2048], P('dp', 'vocab'), may hold values from -150 to 150
- head: bfloat16 [2048, 65536], P(None, 'vocab'), may hold values from -0.375 to 0.375
- mask: int32 [4096], P('dp'), may hold values from 0 to 1
- steps: int32 [32], P('dp'), may hold values from 1 to 8
Outputs:
- divergence: float32 [4096], P('dp')
- hidden_grad: bfloat16 [4096, 2048], P('dp', 'vocab')
All inputs are finite; a program needn't handle non-finite values.
Results may differ from a plain program's by a relative error of at most 0.0051.
Values may be sent and summed in bfloat16 or wider, within the bound.
No kernel may reach another device: no remote copies, remote signals or barrier semaphores. Data moves between devices by JAX's collectives and lax.ppermute only.
A program may use at most 64 MiB of HBM per device.

v0:
```python
import jax
import jax.numpy as jnp
from jax import lax
from jax.sharding import Mesh
from jax.sharding import PartitionSpec as P

LENGTH = 128
STEPS = 8
VOCAB = ("vocab_0", "vocab_1")


def sent_to_all(value, axis):
    copies = jnp.broadcast_to(value, (lax.axis_size(axis), *value.shape))
    return lax.all_to_all(copies, axis, split_axis=0, concat_axis=0, tiled=True)


def taken_together(value, axis):
    everything = sent_to_all(value, axis)
    return jnp.sum(everything, axis=0)


def gather_turned(arrays, axis, dims):
    turned = [jnp.moveaxis(a, dim, 0) for a, dim in zip(arrays, dims)]
    both = jnp.concatenate([t.reshape(len(t), -1) for t in turned], axis=1)
    whole, at, done = (lax.all_gather(both, axis, axis=0, tiled=True), 0, [])
    for t, dim in zip(turned, dims):
        piece = whole[:, at : at + t[0].size].reshape(-1, *t.shape[1:])
        done.append(jnp.moveaxis(piece, 0, dim))
        at += t[0].size
    return tuple(done)


def gathered_once(value, axis):
    leaves = jax.tree.leaves(value)
    order = sorted(range(len(leaves)), key=lambda k: -leaves[k].size)
    width = (1, *leaves[order[0]].shape)[-1]
    lines = [
        jnp.pad(leaves[k].reshape(-1), (0, -leaves[k].size % width)).reshape(-1, width)
        for k in order
    ]
    both, at, found = (sent_to_all(jnp.concatenate(lines), axis), 0, {})
    for k, line in zip(order, lines):
        piece = both[:, at : at + len(line)].reshape(len(both), -1)
        found[k] = piece[:, : leaves[k].size].reshape(-1, *leaves[k].shape)
        at += len(line)
    numbers = iter(range(len(leaves)))
    return jax.tree.map(lambda _: found[next(numbers)], value)


def joined_by_halves(pieces, combine):
    while len(jax.tree.leaves(pieces)[0]) > 1:
        pieces = jax.vmap(combine)(
            *(jax.tree.map(lambda part: part[side::2], pieces) for side in (0, 1))
        )
    return jax.tree.map(lambda part: part[0], pieces)


def merged_2(value, axis, combine):
    pieces = gathered_once(value, axis)
    return joined_by_halves(pieces, combine)


def own_rows(total, axes):
    for axis in axes:
        total = lax.psum_scatter(total, axis, scatter_dimension=0, tiled=True)
    return total


def combine_stats(former, latter):
    student_peak = jnp.maximum(former[0], latter[0])
    teacher_peak = jnp.maximum(former[2], latter[2])
    student_former = jnp.exp(former[0] - student_peak)
    student_latter = jnp.exp(latter[0] - student_peak)
    teacher_former = jnp.exp(former[2] - teacher_peak)
    teacher_latter = jnp.exp(latter[2] - teacher_peak)
    return (
        student_peak,
        former[1] * student_former + latter[1] * student_latter,
        teacher_peak,
        former[3] * teacher_former + latter[3] * teacher_latter,
        former[4] * teacher_former + latter[4] * teacher_latter,
    )


def per_device(student_hidden, teacher_hidden, head, mask, steps):
    rows = mask.shape[0]
    masked = mask.astype(jnp.float32)
    count = taken_together(jnp.sum(masked), "dp")
    factor = jnp.repeat(STEPS / steps.astype(jnp.float32), LENGTH)
    weight = masked * factor * (rows * lax.axis_size("dp") / jnp.maximum(count, 1.0))
    student_full, teacher_full = gather_turned((student_hidden, teacher_hidden), VOCAB, (1, 1))
    student_log = jnp.dot(student_full, head, preferred_element_type=jnp.float32)
    teacher_log = jnp.dot(teacher_full, head, preferred_element_type=jnp.float32)
    student_local = jnp.max(student_log, axis=1)
    teacher_local = jnp.max(teacher_log, axis=1)
    student_exp = jnp.exp(student_log - student_local[:, None])
    teacher_exp = jnp.exp(teacher_log - teacher_local[:, None])
    student_sum = jnp.sum(student_exp, axis=1)
    teacher_sum = jnp.sum(teacher_exp, axis=1)
    cross_sum = jnp.sum(teacher_exp * (teacher_log - student_log), axis=1)
    merged = merged_2(
        (student_local, student_sum, teacher_local, teacher_sum, cross_sum), VOCAB, combine_stats
    )
    student_peak, student_total, teacher_peak, teacher_total, cross = merged
    divergence = (
        cross / teacher_total
        - (teacher_peak + jnp.log(teacher_total))
        + (student_peak + jnp.log(student_total))
    )
    student_prob = student_exp * (jnp.exp(student_local - student_peak) / student_total)[:, None]
    teacher_prob = teacher_exp * (jnp.exp(teacher_local - teacher_peak) / teacher_total)[:, None]
    slopes = (weight[:, None] * (student_prob - teacher_prob)).astype(jnp.bfloat16)
    summed = own_rows(
        lax.dot_general(head, slopes, (((1,), (1,)), ((), ())), preferred_element_type=jnp.float32),
        VOCAB,
    )
    hidden_grad = summed.T.astype(jnp.bfloat16)
    return (divergence, hidden_grad)


def solution(mesh):
    torus = Mesh(mesh.devices.reshape(mesh.shape["dp"], 4, 8), ("dp", "vocab_0", "vocab_1"))
    in_specs = (P("dp", VOCAB), P("dp", VOCAB), P(None, VOCAB), P("dp"), P("dp"))
    out_specs = (P("dp"), P("dp", VOCAB))
    return jax.shard_map(
        per_device, mesh=torus, in_specs=in_specs, out_specs=out_specs, check_vma=False
    )
```

profile of v0, /device:TPU:2, one launch (start us, length us, event | category | flops | bytes accessed | tf_op | source)
XLA Modules:
  0.0 246.0 jit_solution(11770091090711310746)
XLA Ops:
  7.2 0.0 all-gather.2.cloned.1.call-start
  7.2 1.5 pad_maximum_fusion
  8.7 0.0 all-gather.2.cloned.1.call-update
  8.8 1.3 convert_reduce_fusion
  10.1 1.2 broadcast_in_dim.16
  11.3 4.5 %all-to-all-start.1 = ((f32[8,1,1]{2,1,0:T(1,128)}), f32[8,1,1]{2,1,0:T(1,128)S(1)}, u32[]{:S(2)}, u32[]{:S(2)}) async-start(f32[8,1,1]{2,1,0:T(1,128)} %broadcast_in_dim.16), calls=%async_computation.1 | async-start | bytes 8192 | tf_op jit(solution)/shard_map/all_to_all | solution.py:14
  15.8 78.2 %all-gather.2.cloned.1.call-done = bf16[2048,1024]{1,0:T(8,128)(2,1)} async-done(((bf16[64,1024]{1,0:T(8,128)(2,1)}), bf16[2048,1024]{1,0:T(8,128)(2,1)}) %all-gather.2.cloned.1.call-update) | async-done | bytes 4194320 | tf_op jit(solution)/shard_map/all_gather | solution.py:25
  94.0 0.0 copy-start.3
  94.0 7.9 %fusion.17 = (f32[512]{0:T(512)S(1)}, f32[512,2048]{1,0:T(8,128)S(1)}) fusion(bf16[2048,2048]{1,0:T(8,128)(2,1)} %param.7, bf16[2048,1024]{1,0:T(8,128)(2,1)} %all-gather.2.cloned.1.call-done), kind=kOutput, calls=%fused_computation.65 | convolution fusion | flops 4296015360 | bytes 14682112 | tf_op jit(solution)/shard_map/dot_general | solution.py:93
  101.9 0.0 copy-done.3
  101.9 0.0 copy-start
  101.9 8.7 %fusion.16 = (f32[512]{0:T(512)S(1)}, f32[512,2048]{1,0:T(8,128)S(1)}) fusion(bf16[2048,2048]{1,0:T(8,128)(2,1)} %param.7, bf16[2048,1024]{1,0:T(8,128)(2,1)S(1)} %copy-done.3), kind=kOutput, calls=%fused_computation.64 | convolution fusion | flops 4296015360 | bytes 14682112 | tf_op jit(solution)/shard_map/dot_general | solution.py:92
  110.6 0.0 copy-start.1
  110.6 0.0 copy-done
  110.6 0.0 copy-start.4
  110.6 0.0 copy-start.2
  110.7 2.1 multiply_reduce_fusion
  112.8 0.0 copy-done.1
  112.8 0.0 all-to-all-done.1
  112.8 0.9 broadcast_in_dim.6
  113.7 6.9 %all-to-all-start = ((f32[32,5,512]{2,1,0:T(8,128)}), f32[32,5,512]{2,1,0:T(8,128)S(1)}, u32[]{:S(2)}, u32[]{:S(2)}) async-start(f32[32,5,512]{2,1,0:T(8,128)} %broadcast_in_dim.6), calls=%async_computation | async-start | bytes 1048576 | tf_op jit(solution)/shard_map/all_to_all | solution.py:14
  120.6 0.0 reduce-scatter.5.cloned.1.call-start
  120.7 0.0 copy-done.4
  120.7 0.6 reduce_sum.49
  122.0 0.0 copy-done.2
  122.0 0.1 fusion.14
  122.1 11.6 %all-to-all-done = f32[32,5,512]{2,1,0:T(8,128)S(1)} async-done(((f32[32,5,512]{2,1,0:T(8,128)}), f32[32,5,512]{2,1,0:T(8,128)S(1)}, u32[]{:S(2)}, u32[]{:S(2)}) %all-to-all-start) | async-done | bytes 327712 | tf_op jit(solution)/shard_map/all_to_all | solution.py:14
  133.6 0.2 fusion.15
  135.1 0.6 exponential_divide_fusion.1
  135.7 12.8 %convolution_bitcast_fusion = f32[2048,512]{0,1:T(8,128)} fusion(bf16[2048,2048]{1,0:T(8,128)(2,1)} %param.7, f32[512,2048]{1,0:T(8,128)} %copy-done, f32[512,2048]{1,0:T(8,128)} %copy-done.1, f32[512]{0:T(512)S(1)} %get-tuple-element.40, f32[512]{0:T(512)S(1)} %get-tuple-element.38, f32[512]{0:T(512)S(1)} %fusion.14, f32[512]{0:T(512)S(1)} %get-tuple-element.43, ...), kind=kOutput, calls=%fused_computation.6 | convolution fusion | flops 4302307328 | bytes 20981760 | tf_op jit(solution)/shard_map/dot_general | solution.py:114
  148.5 0.0 reduce-scatter.5.cloned.1.call-update
  148.5 0.0 reduce-scatter.7.cloned.1.call-start
  148.6 46.3 %reduce-scatter.5.cloned.1.call-done = f32[512,512]{0,1:T(8,128)} async-done(((f32[2048,512]{0,1:T(8,128)}), f32[512,512]{0,1:T(8,128)}) %reduce-scatter.5.cloned.1.call-update) | async-done | bytes 1048592 | tf_op jit(solution)/shard_map/reduce_scatter | solution.py:65
  194.9 2.6 %copy.24 = f32[512,512]{1,0:T(8,128)} copy(f32[512,512]{0,1:T(8,128)} %reduce-scatter.5.cloned.1.call-done) | data formatting | bytes 2097152
  197.5 0.0 reduce-scatter.7.cloned.1.call-update
  197.5 40.2 %reduce-scatter.7.cloned.1.call-done = f32[64,512]{1,0:T(8,128)} async-done(((f32[512,512]{1,0:T(8,128)}), f32[64,512]{1,0:T(8,128)}) %reduce-scatter.7.cloned.1.call-update) | async-done | bytes 131088
  237.7 1.0 copy.25
  238.7 0.7 copy.23
  (60 shorter events, 1.2 us)
Async XLA Ops:
  7.2 86.8 %all-gather.2.cloned.1.call-start = ((), (), s32[]{:S(2)}) async-start(), calls=%async_computation.4 | async-start | bytes 4325376 | tf_op jit(solution)/shard_map/all_gather | solution.py:25
  11.3 101.5 %all-to-all-start.1 = ((f32[8,1,1]{2,1,0:T(1,128)}), f32[8,1,1]{2,1,0:T(1,128)S(1)}, u32[]{:S(2)}, u32[]{:S(2)}) async-start(f32[8,1,1]{2,1,0:T(1,128)} %broadcast_in_dim.16), calls=%async_computation.1 | async-start | bytes 8192 | tf_op jit(solution)/shard_map/all_to_all | solution.py:14
  94.0 7.9 %copy-start.3 = (bf16[2048,1024]{1,0:T(8,128)(2,1)S(1)}, bf16[2048,1024]{1,0:T(8,128)(2,1)}, u32[]{:S(2)}) copy-start(bf16[2048,1024]{1,0:T(8,128)(2,1)} %all-gather.2.cloned.1.call-done) | copy-start | bytes 12582916
  101.9 8.7 %copy-start = (f32[512,2048]{1,0:T(8,128)}, f32[512,2048]{1,0:T(8,128)S(1)}, u32[]{:S(2)}) copy-start(f32[512,2048]{1,0:T(8,128)S(1)} %get-tuple-element.44) | copy-start | bytes 12582916
  110.6 2.2 copy-start.1
  110.6 10.0 %copy-start.4 = (s32[4]{0:T(128)S(1)}, s32[4]{0:T(128)}, u32[]{:S(2)}) copy-start(s32[4]{0:T(128)} %param.9) | copy-start | bytes 52
  110.6 11.3 %copy-start.2 = (s32[512]{0:T(512)S(1)}, s32[512]{0:T(512)}, u32[]{:S(2)}) copy-start(s32[512]{0:T(512)} %param.8) | copy-start | bytes 6148
  113.7 19.9 %all-to-all-start = ((f32[32,5,512]{2,1,0:T(8,128)}), f32[32,5,512]{2,1,0:T(8,128)S(1)}, u32[]{:S(2)}, u32[]{:S(2)}) async-start(f32[32,5,512]{2,1,0:T(8,128)} %broadcast_in_dim.6), calls=%async_computation | async-start | bytes 1048576 | tf_op jit(solution)/shard_map/all_to_all | solution.py:14
  120.6 74.3 %reduce-scatter.5.cloned.1.call-start = ((), (), s32[]{:S(2)}) async-start(), calls=%async_computation.5 | async-start | bytes 5242880 | tf_op jit(solution)/shard_map/reduce_scatter | solution.py:65
  148.5 89.1 %reduce-scatter.7.cloned.1.call-start = ((), (), s32[]{:S(2)}) async-start(), calls=%async_computation.6 | async-start | bytes 1179648
Sparse Core Ops, SparseCore 0:
  10.6 83.4 all-gather.1
  148.7 46.1 reduce-scatter.4
  197.6 40.0 reduce-scatter.6
where the time goes:
time: 246 us
  waiting for transfers between devices  176 us (72%)
  matrix products  29.4 us (12%)
  between operations  14.7 us (6%)
  starting transfers between devices  11.5 us (5%)
  local copies, waits for them, and re-layouts  7.61 us (3%)
  other arithmetic  6.51 us (3%)
    all_gather x1, waiting for transfers between devices, gather_turned(): whole, at, done = (lax.all_gather(both, axis, axis=0, tiled=True), 0, [])  78.2 us
    reduce_scatter x1, waiting for transfers between devices, own_rows(): total = lax.psum_scatter(total, axis, scatter_dimension=0, tiled=True)  46.3 us
    unnamed x4, waiting for transfers between devices  40.2 us
    dot_general x1, matrix products, per_device(): lax.dot_general(head, slopes, (((1,), (1,)), ((), ())), preferred_element...  12.8 us
    all_to_all x2, waiting for transfers between devices, sent_to_all(): return lax.all_to_all(copies, axis, split_axis=0, concat_axis=0, tiled=True)  11.6 us
    all_to_all x2, starting transfers between devices, sent_to_all(): return lax.all_to_all(copies, axis, split_axis=0, concat_axis=0, tiled=True)  11.3 us
    dot_general x1, matrix products, per_device(): jnp.dot(student_full, head, preferred_element_type=jnp.float32)  8.68 us
    dot_general x1, matrix products, per_device(): jnp.dot(teacher_full, head, preferred_element_type=jnp.float32)  7.88 us
  transfers between devices with their start and end apart: 5, of which 4 were waited for; matrix products, arithmetic and copies ran while one was open for 9% of the time, Pallas kernels for 0%

commit v1 on v0

--- a/solution.py
+++ b/solution.py
@@ -22,7 +22,13 @@
 def gather_turned(arrays, axis, dims):
     turned = [jnp.moveaxis(a, dim, 0) for a, dim in zip(arrays, dims)]
     both = jnp.concatenate([t.reshape(len(t), -1) for t in turned], axis=1)
-    whole, at, done = (lax.all_gather(both, axis, axis=0, tiled=True), 0, [])
+    whole, at, done = (
+        jnp.concatenate(
+            lax.all_to_all(jnp.stack([both] * lax.axis_size(axis)), axis, 0, 0), axis=0
+        ),
+        0,
+        [],
+    )
     for t, dim in zip(turned, dims):
         piece = whole[:, at : at + t[0].size].reshape(-1, *t.shape[1:])
         done.append(jnp.moveaxis(piece, 0, dim))

time: 246 us -> 280 us (1.14)
  waiting for transfers between devices: 176 us -> 195 us
  starting transfers between devices: 11.5 us -> 23.9 us
    all_to_all x0 -> x1, waiting for transfers between devices: none -> 93.9 us  [gather_turned(): lax.all_to_all(jnp.stack([both] * lax.axis_size(axis)), axis, 0, 0)]
    all_gather x1 -> x0, waiting for transfers between devices: 78.2 us -> none  [gather_turned(): whole, at, done = (lax.all_gather(both, axis, axis=0, tiled=True), 0, [])]
    all_to_all x0 -> x1, starting transfers between devices: none -> 11.8 us  [gather_turned(): lax.all_to_all(jnp.stack([both] * lax.axis_size(axis)), axis, 0, 0)]
    all_to_all x2, waiting for transfers between devices: 11.6 us -> 14.8 us  [sent_to_all(): return lax.all_to_all(copies, axis, split_axis=0, concat_axis=0, tiled=True)]
    unnamed x4 -> x3, waiting for transfers between devices: 40.2 us -> 40.2 us
  transfers between devices with their start and end apart: 5 -> 5, of which waited for: 4 -> 4; matrix products, arithmetic and copies ran while one was open for 9% -> 7% of each run, Pallas kernels for 0% -> 0%
where the time goes in v1:
time: 280 us; the launch traced here: 279 us
  waiting for transfers between devices  195 us (70%)
  matrix products  29.8 us (11%)
  starting transfers between devices  23.9 us (9%)
  between operations  15 us (5%)
  local copies, waits for them, and re-layouts  10.1 us (4%)
  other arithmetic  5.18 us (2%)
    all_to_all x1, waiting for transfers between devices, gather_turned(): lax.all_to_all(jnp.stack([both] * lax.axis_size(axis)), axis, 0, 0)  93.9 us
    reduce_scatter x1, waiting for transfers between devices, own_rows(): total = lax.psum_scatter(total, axis, scatter_dimension=0, tiled=True)  46.4 us
    unnamed x3, waiting for transfers between devices  40.2 us
    all_to_all x2, waiting for transfers between devices, sent_to_all(): return lax.all_to_all(copies, axis, split_axis=0, concat_axis=0, tiled=True)  14.8 us
    dot_general x1, matrix products, per_device(): lax.dot_general(head, slopes, (((1,), (1,)), ((), ())), preferred_element...  12.8 us
    all_to_all x2, starting transfers between devices, sent_to_all(): return lax.all_to_all(copies, axis, split_axis=0, concat_axis=0, tiled=True)  12 us
    all_to_all x1, starting transfers between devices, gather_turned(): lax.all_to_all(jnp.stack([both] * lax.axis_size(axis)), axis, 0, 0)  11.8 us
    dot_general x1, matrix products, per_device(): jnp.dot(student_full, head, preferred_element_type=jnp.float32)  9.26 us
  transfers between devices with their start and end apart: 5, of which 4 were waited for; matrix products, arithmetic and copies ran while one was open for 7% of the time, Pallas kernels for 0%

profile of v1, /device:TPU:2, one launch (start us, length us, event | category | flops | bytes accessed | tf_op | source)
XLA Modules:
  0.0 279.3 jit_solution(3821326270522966472)
XLA Ops:
  7.2 0.9 pad_maximum_fusion
  8.0 2.5 stack.2
  10.5 0.0 copy-start.2
  10.5 11.8 %all-to-all-start = ((bf16[32,64,1024]{2,1,0:T(8,128)(2,1)}), bf16[32,64,1024]{2,1,0:T(8,128)(2,1)}, u32[]{:S(2)}, u32[]{:S(2)}) async-start(bf16[32,64,1024]{2,1,0:T(8,128)(2,1)} %stack.2), calls=%async_computation | async-start | bytes 8388608 | tf_op jit(solution)/shard_map/all_to_all | solution.py:27
  22.3 0.0 copy-done.2
  22.3 0.6 convert_reduce_fusion
  22.9 93.9 %all-to-all-done = bf16[32,64,1024]{2,1,0:T(8,128)(2,1)} async-done(((bf16[32,64,1024]{2,1,0:T(8,128)(2,1)}), bf16[32,64,1024]{2,1,0:T(8,128)(2,1)}, u32[]{:S(2)}, u32[]{:S(2)}) %all-to-all-start) | async-done | bytes 4194336 | tf_op jit(solution)/shard_map/all_to_all | solution.py:27
  116.8 1.2 broadcast_in_dim.16
  118.1 4.5 %all-to-all-start.2 = ((f32[8,1,1]{2,1,0:T(1,128)}), f32[8,1,1]{2,1,0:T(1,128)S(1)}, u32[]{:S(2)}, u32[]{:S(2)}) async-start(f32[8,1,1]{2,1,0:T(1,128)} %broadcast_in_dim.16), calls=%async_computation.2 | async-start | bytes 8192 | tf_op jit(solution)/shard_map/all_to_all | solution.py:14
  122.5 7.8 %fusion.17 = (f32[512]{0:T(512)S(1)}, f32[512,2048]{1,0:T(8,128)S(1)}) fusion(bf16[2048,2048]{1,0:T(8,128)(2,1)} %param.7, bf16[2048,1024]{1,0:T(8,128)(2,1)} %bitcast.2), kind=kOutput, calls=%fused_computation.65 | convolution fusion | flops 4296015360 | bytes 14682112 | tf_op jit(solution)/shard_map/dot_general | solution.py:99
  130.3 0.0 copy-start
  130.3 9.3 %fusion.16 = (f32[512]{0:T(512)S(1)}, f32[512,2048]{1,0:T(8,128)S(1)}) fusion(bf16[2048,2048]{1,0:T(8,128)(2,1)} %param.7, bf16[2048,1024]{1,0:T(8,128)(2,1)} %bitcast.2), kind=kOutput, calls=%fused_computation.64 | convolution fusion | flops 4296015360 | bytes 14682112 | tf_op jit(solution)/shard_map/dot_general | solution.py:98
  139.6 0.0 copy-start.1
  139.6 0.0 copy-done
  139.6 0.0 copy-start.3
  139.6 2.1 multiply_reduce_fusion
  141.8 0.0 copy-done.1
  141.8 0.0 all-to-all-done.2
  141.8 0.9 broadcast_in_dim.6
  142.7 7.5 %all-to-all-start.1 = ((f32[32,5,512]{2,1,0:T(8,128)}), f32[32,5,512]{2,1,0:T(8,128)S(1)}, u32[]{:S(2)}, u32[]{:S(2)}) async-start(f32[32,5,512]{2,1,0:T(8,128)} %broadcast_in_dim.6), calls=%async_computation.1 | async-start | bytes 1048576 | tf_op jit(solution)/shard_map/all_to_all | solution.py:14
  150.2 0.0 reduce-scatter.5.cloned.1.call-start
  150.3 0.0 copy-done.3
  150.3 0.6 reduce_sum.49
  151.6 0.1 fusion.14
  151.7 14.8 %all-to-all-done.1 = f32[32,5,512]{2,1,0:T(8,128)S(1)} async-done(((f32[32,5,512]{2,1,0:T(8,128)}), f32[32,5,512]{2,1,0:T(8,128)S(1)}, u32[]{:S(2)}, u32[]{:S(2)}) %all-to-all-start.1) | async-done | bytes 327712 | tf_op jit(solution)/shard_map/all_to_all | solution.py:14
  166.4 0.2 fusion.15
  168.0 0.6 exponential_divide_fusion.1
  168.5 12.8 %convolution_bitcast_fusion = f32[2048,512]{0,1:T(8,128)} fusion(bf16[2048,2048]{1,0:T(8,128)(2,1)} %param.7, f32[512,2048]{1,0:T(8,128)} %copy-done, f32[512,2048]{1,0:T(8,128)} %copy-done.1, f32[512]{0:T(512)S(1)} %get-tuple-element.40, f32[512]{0:T(512)S(1)} %get-tuple-element.38, f32[512]{0:T(512)S(1)} %fusion.14, f32[512]{0:T(512)S(1)} %get-tuple-element.43, ...), kind=kOutput, calls=%fused_computation.6 | convolution fusion | flops 4302307328 | bytes 20981760 | tf_op jit(solution)/shard_map/dot_general | solution.py:120
  181.4 0.0 reduce-scatter.5.cloned.1.call-update
  181.4 0.0 reduce-scatter.7.cloned.1.call-start
  181.4 46.4 %reduce-scatter.5.cloned.1.call-done = f32[512,512]{0,1:T(8,128)} async-done(((f32[2048,512]{0,1:T(8,128)}), f32[512,512]{0,1:T(8,128)}) %reduce-scatter.5.cloned.1.call-update) | async-done | bytes 1048592 | tf_op jit(solution)/shard_map/reduce_scatter | solution.py:71
  227.9 2.6 copy.24
  230.5 0.0 reduce-scatter.7.cloned.1.call-update
  230.5 40.2 %reduce-scatter.7.cloned.1.call-done = f32[64,512]{1,0:T(8,128)} async-done(((f32[512,512]{1,0:T(8,128)}), f32[64,512]{1,0:T(8,128)}) %reduce-scatter.7.cloned.1.call-update) | async-done | bytes 131088
  270.7 1.0 copy.25
  271.7 0.7 copy.23
  (60 shorter events, 1.2 us)
Async XLA Ops:
  10.5 11.8 %copy-start.2 = (s32[512]{0:T(512)S(1)}, s32[512]{0:T(512)}, u32[]{:S(2)}) copy-start(s32[512]{0:T(512)} %param.8) | copy-start | bytes 6148
  10.5 106.3 %all-to-all-start = ((bf16[32,64,1024]{2,1,0:T(8,128)(2,1)}), bf16[32,64,1024]{2,1,0:T(8,128)(2,1)}, u32[]{:S(2)}, u32[]{:S(2)}) async-start(bf16[32,64,1024]{2,1,0:T(8,128)(2,1)} %stack.2), calls=%async_computation | async-start | bytes 8388608 | tf_op jit(solution)/shard_map/all_to_all | solution.py:27
  118.1 23.7 %all-to-all-start.2 = ((f32[8,1,1]{2,1,0:T(1,128)}), f32[8,1,1]{2,1,0:T(1,128)S(1)}, u32[]{:S(2)}, u32[]{:S(2)}) async-start(f32[8,1,1]{2,1,0:T(1,128)} %broadcast_in_dim.16), calls=%async_computation.2 | async-start | bytes 8192 | tf_op jit(solution)/shard_map/all_to_all | solution.py:14
  130.3 9.3 %copy-start = (f32[512,2048]{1,0:T(8,128)}, f32[512,2048]{1,0:T(8,128)S(1)}, u32[]{:S(2)}) copy-start(f32[512,2048]{1,0:T(8,128)S(1)} %get-tuple-element.44) | copy-start | bytes 12582916
  139.6 2.2 copy-start.1
  139.6 10.7 %copy-start.3 = (s32[4]{0:T(128)S(1)}, s32[4]{0:T(128)}, u32[]{:S(2)}) copy-start(s32[4]{0:T(128)} %param.9) | copy-start | bytes 52
  142.7 23.8 %all-to-all-start.1 = ((f32[32,5,512]{2,1,0:T(8,128)}), f32[32,5,512]{2,1,0:T(8,128)S(1)}, u32[]{:S(2)}, u32[]{:S(2)}) async-start(f32[32,5,512]{2,1,0:T(8,128)} %broadcast_in_dim.6), calls=%async_computation.1 | async-start | bytes 1048576 | tf_op jit(solution)/shard_map/all_to_all | solution.py:14
  150.2 77.6 %reduce-scatter.5.cloned.1.call-start = ((), (), s32[]{:S(2)}) async-start(), calls=%async_computation.5 | async-start | bytes 5242880 | tf_op jit(solution)/shard_map/reduce_scatter | solution.py:71
  181.4 89.3 %reduce-scatter.7.cloned.1.call-start = ((), (), s32[]{:S(2)}) async-start(), calls=%async_computation.6 | async-start | bytes 1179648
Sparse Core Ops, SparseCore 0:
  181.5 46.3 reduce-scatter.4
  230.6 40.0 reduce-scatter.6
